TPU v7x, 32 devices: a whole 2x2x4 slice. The times are simulated.
32 devices in a mesh: node: 16 (over z, x, core), tone: 2 (over y).
Axes of the slice: x: 2, y: 2, z: 4, core: 2. Of those that a mesh axis runs over, the one named last changes fastest.
Arguments:
- voltages: float32 [32, 32, 16384], P(None, 'tone', 'node'), may hold values from -6 to 6
- source: float32 [32, 32, 16384], P(None, 'tone', 'node'), may hold values from -6 to 6
- coupling: float32 [128, 7, 128, 128], P('node'), may hold values from -0.1875 to 0.1875
- band_code: int32 [7], replicated, may hold values from 0 to 6, each once
- active: int32 [128, 7], P('node'), may hold values 0 or 1
- cap: float32 [16384], P('node'), may hold values from 0.5 to 2
- damp: float32 [32, 32], P(None, 'tone'), may hold values from 0.5 to 4
- kind: int32 [16384], P('node'), may hold values from 0 to 3
- type_params: float32 [3, 4], replicated, may hold values from 0.3 to 2
Outputs:
- new_voltages: float32 [32, 32, 16384], P(None, 'tone', 'node')
- remaining: float32 [32, 32, 16384], P(None, 'tone', 'node')
Inputs may be any that keep to these rules, and one draw needn't show every extreme that they name: band_code holds each of 0 to 6 once, so the bands reach every block offset from -3 to 3.
All inputs are finite; a program needn't handle non-finite values. No bound on the sum of `active` on one device may be relied on, other than what follows from the above.
Results may differ from a plain program's by a relative error of at most 0.0003.
Values sent between devices are 32-bit elements; how exact they have to be, the bound alone decides.
No kernel may reach another device: no remote copies, remote signals or barrier semaphores. Data moves between devices by JAX's collectives and lax.ppermute only.
A program may use at most 128 MiB of HBM per device.

v0:
```python
import math
import jax
import jax.numpy as jnp
from jax import lax
from jax.sharding import PartitionSpec as P

K1 = 32
K2 = 32
NB = 128
HALO_B = 3
NOFF = 7
M = 4
NTYPES = 4
HIGH = lax.Precision.HIGHEST


def extended(value, sides, width):
    for axis, dim in sides:
        count, length = (lax.axis_size(axis), value.shape[dim])
        up = [(i, (i + 1) % count) for i in range(count - 1)]
        down = [(j, i) for i, j in up]
        last = lax.slice_in_dim(value, length - width, length, axis=dim)
        leading = lax.slice_in_dim(value, 0, width, axis=dim)
        before = lax.ppermute(last, axis, up)
        after = lax.ppermute(leading, axis, down)
        value = jnp.concatenate([before, value, after], axis=dim)
    return value


def hartley(count):
    grid = jnp.arange(count, dtype=jnp.int32)
    phase = grid[:, None] * grid[None, :] % count
    angle = phase.astype(jnp.float32) * (2.0 * math.pi / count)
    return (jnp.cos(angle) + jnp.sin(angle)) / math.sqrt(count)


def along_first(table, field):
    return jnp.einsum("tk,kqn->tqn", table, field, precision=HIGH)


def along_second(table, field):
    return jnp.einsum("sq,tqn->tsn", table, field, precision=HIGH)


def band_matrix(masked, band_code, nodes):
    blocks = nodes // NB
    reach = HALO_B * NB
    offsets = jnp.arange(NOFF, dtype=jnp.int32)
    select = (offsets[:, None] == band_code[None, :]).astype(jnp.float32)
    per_offset = jnp.einsum("oj,bjsc->obsc", select, masked, precision=HIGH)
    diagonal = jnp.eye(blocks, dtype=jnp.float32)
    operator = jnp.zeros((nodes + 2 * reach, nodes), dtype=jnp.float32)
    for offset in range(NOFF):
        placed = jnp.einsum("bsc,bd->bcds", per_offset[offset], diagonal).reshape(nodes, nodes)
        operator = operator.at[offset * NB : offset * NB + nodes].add(placed)
    return operator


def couple(field, operator, scale):
    reach = HALO_B * NB
    padded = extended(field, (("node", 2),), reach)
    rows = field.shape[0] * field.shape[1]
    term = jnp.dot(padded.reshape(rows, padded.shape[2]), operator, precision=HIGH)
    return scale * field + term.reshape(field.shape)


def small_solve(gram, rhs):
    lower = jnp.linalg.cholesky(gram)
    count = rhs.shape[0]
    forward = []
    for index in range(count):
        total = rhs[index]
        for other in range(index):
            total = total - lower[index, other] * forward[other]
        forward.append(total / lower[index, index])
    backward = [None] * count
    for index in reversed(range(count)):
        total = forward[index]
        for other in range(index + 1, count):
            total = total - lower[other, index] * backward[other]
        backward[index] = total / lower[index, index]
    return jnp.stack(backward)


def per_device(voltages, source, coupling, band_code, active, cap, damp, kind, type_params):
    first = hartley(K1)
    second = hartley(K2)
    onehot = (kind[None, :] == jnp.arange(NTYPES, dtype=jnp.int32)[:, None]).astype(jnp.float32)
    per_node = jnp.dot(type_params, onehot, precision=HIGH)
    masked = coupling * active[:, :, None, None].astype(jnp.float32)
    operator = band_matrix(masked, band_code, voltages.shape[2])
    scale = damp[:, :, None] * cap[None, None, :]

    def to_time(field):
        moved = lax.all_to_all(
            along_first(first, field), "tone", split_axis=0, concat_axis=1, tiled=True
        )
        return along_second(second, moved)

    def to_freq(field):
        moved = lax.all_to_all(
            along_second(second, field), "tone", split_axis=1, concat_axis=0, tiled=True
        )
        return along_first(first, moved)

    linear, amplitude, sharpness = (per_node[0], per_node[1], per_node[2])
    wave = to_time(voltages)
    bend = jnp.tanh(sharpness * wave)
    current = linear * wave + amplitude * bend
    slope = linear + amplitude * sharpness * (1.0 - bend * bend)
    start = source - couple(voltages, operator, scale) - to_freq(current)
    beta = jnp.sqrt(lax.psum(jnp.sum(start * start), ("node", "tone")))
    basis = [start / beta]
    hessen = jnp.zeros((M + 1, M), dtype=jnp.float32)
    for column in range(M):
        jacobian_field = basis[column]
        image = couple(jacobian_field, operator, scale) + to_freq(slope * to_time(jacobian_field))
        local_terms = jnp.stack([jnp.sum(vector * image) for vector in basis])
        projected = lax.psum(local_terms, ("node", "tone"))
        for index in range(len(basis)):
            image = image - projected[index] * basis[index]
        length = jnp.sqrt(lax.psum(jnp.sum(image * image), ("node", "tone")))
        hessen = hessen.at[: column + 1, column].set(projected)
        hessen = hessen.at[column + 1, column].set(length)
        basis.append(image / length)
    gram = jnp.dot(hessen.T, hessen, precision=HIGH)
    coeffs = small_solve(gram, beta * hessen[0])
    fitted = jnp.dot(hessen, coeffs, precision=HIGH)
    update = coeffs[0] * basis[0]
    for index in range(1, M):
        update = update + coeffs[index] * basis[index]
    remaining = start
    for index in range(M + 1):
        remaining = remaining - fitted[index] * basis[index]
    return (voltages + update, remaining)


def solution(mesh):
    placed = (
        P(None, "tone", "node"),
        P(None, "tone", "node"),
        P("node", None, None, None),
        P(),
        P("node", None),
        P("node"),
        P(None, "tone"),
        P("node"),
        P(),
    )
    return jax.shard_map(
        per_device,
        mesh=mesh,
        in_specs=placed,
        out_specs=(P(None, "tone", "node"), P(None, "tone", "node")),
        check_vma=False,
    )
```

profile of v0, /device:TPU:0, one launch (start us, length us, event | category | flops | bytes accessed | tf_op | source)
XLA Modules:
  0.0 942.5 jit_solution(3432726177361847667)
XLA Ops:
  0.6 4.6 fusion.72
  7.8 5.0 all-to-all-start
  21.3 4.1 fusion.16
  25.4 4.2 fusion.273
  33.9 9.7 %broadcast_multiply_fusion = (f32[8,8,128,128]{2,1,3,0:T(8,128)}, f32[8,8,128,128]{2,1,3,0:T(8,128)}, f32[8,8,128,128]{2,1,3,0:T(8,128)}, f32[8,8,128,128]{2,1,3...) fusion(f32[8,128,128]{1,2,0:T(8,128)} %copy.111, ...), kind=kLoop, calls=%fused_computation.116 | loop fusion | flops 7340032 | bytes 33030400 | tf_op jit(solution)/shard_map/bsc,bd->bcds/dot_general | solution.py:54
  46.8 6.3 scatter-add.24
  53.2 5.8 fusion.15
  59.0 5.9 fusion.14
  64.9 5.9 fusion.13
  70.8 5.7 fusion.12
  86.0 3.8 all-to-all-start.1
  89.8 7.2 fusion.11
  97.0 5.7 fusion.10
  102.7 12.3 %all-to-all-done.1 = f32[16,32,1024]{2,0,1:T(8,128)S(1)} async-done(((f32[16,32,1024]{2,0,1:T(8,128)}), f32[16,32,1024]{2,0,1:T(8,128)S(1)}, u32[]{:S(2)}, u32[]{:S(2)}) %all-to-all-start.1) | async-done | bytes 2097184 | tf_op jit(solution)/shard_map/all_to_all | solution.py:101
  117.3 17.0 %multiply_reduce_fusion.14 = (f32[]{:T(128)}, f32[32,16,1024]{2,1,0:T(8,128)S(1)}) fusion(f32[32,16,1024]{2,0,1:T(8,128)S(1)} %fusion.146, f32[32,16,1024]{2,1,0:T(8,128)S(1)} %copy-done.30, f32[1792,1024]{1,0:T(8,128)} %fusion.10, f32[32,16,384]{2,1,0:T(8,128)} %collective-permute-done.1, f32[32,16,1024]{2,1,0:T(8,128)S(1)} %copy-done.16, ...), kind=kOutput, calls=%fused_computation.111 | convolution fusion | flops 11279794176 | bytes 17307652 | tf_op jit(solution)/shard_map/dot_general | solution.py:63
  134.3 42.4 %psum.63 = f32[]{:T(128)} all-reduce(f32[]{:T(128)} %get-tuple-element.256), channel_id=1, replica_groups=mesh['node'=16,'tone'=2] {'node','tone'}, use_global_device_ids=true, to_apply=%region_1.2 | all-reduce | flops 1 | bytes 8 | tf_op jit(solution)/shard_map/psum | solution.py:112
  183.2 5.0 all-to-all-start.2
  188.2 25.1 %all-to-all-done.2 = f32[32,16,1024]{2,1,0:T(8,128)} async-done(((f32[32,16,1024]{2,1,0:T(8,128)}), f32[32,16,1024]{2,1,0:T(8,128)}, u32[]{:S(2)}, u32[]{:S(2)}) %all-to-all-start.2) | async-done | bytes 2097184 | tf_op jit(solution)/shard_map/all_to_all | solution.py:95
  222.5 4.8 all-to-all-start.3
  233.6 17.5 %all-to-all-done.3 = f32[16,32,1024]{2,0,1:T(8,128)} async-done(((f32[16,32,1024]{2,0,1:T(8,128)}), f32[16,32,1024]{2,0,1:T(8,128)}, u32[]{:S(2)}, u32[]{:S(2)}) %all-to-all-start.3) | async-done | bytes 2097184 | tf_op jit(solution)/shard_map/all_to_all | solution.py:101
  254.8 17.5 %multiply_reduce_fusion.13 = (f32[]{:T(128)}, f32[32,16,1024]{2,1,0:T(8,128)}) fusion(f32[32,16,1024]{2,1,0:T(8,128)S(1)} %get-tuple-element.257, f32[]{:T(128)S(6)} %sqrt.15, f32[32,16,1024]{2,0,1:T(8,128)S(1)} %fusion.140, f32[1792,1024]{1,0:T(8,128)} %fusion.10, f32[32,16,384]{2,1,0:T(8,128)} %collective-permute-done.3, ...), kind=kOutput, calls=%fused_computation.110 | convolution fusion | flops 11279794176 | bytes 17307656 | tf_op jit(solution)/shard_map/dot_general | solution.py:63
  272.3 38.9 %psum.64 = f32[1]{0:T(128)} all-reduce(f32[1]{0:T(128)} %bitcast.38), channel_id=1, replica_groups=mesh['node'=16,'tone'=2] {'node','tone'}, use_global_device_ids=true, to_apply=%region_3.4 | all-reduce | flops 1 | bytes 8 | tf_op jit(solution)/shard_map/psum | solution.py:119
  311.2 3.4 multiply_reduce_fusion.12
  314.6 41.2 %psum.65 = f32[]{:T(128)} all-reduce(f32[]{:T(128)} %multiply_reduce_fusion.12), channel_id=1, replica_groups=mesh['node'=16,'tone'=2] {'node','tone'}, use_global_device_ids=true, to_apply=%region_5.6 | all-reduce | flops 1 | bytes 8 | tf_op jit(solution)/shard_map/psum | solution.py:122
  363.6 27.1 %all_to_all.180 = f32[32,16,1024]{2,1,0:T(8,128)S(1)} all-to-all(f32[32,16,1024]{2,1,0:T(8,128)S(1)} %copy.125), channel_id=1, replica_groups=mesh['node'=16,'tone'=2] {'tone'}, dimensions={0} | all-to-all | bytes 4194304 | tf_op jit(solution)/shard_map/all_to_all | solution.py:95
  398.4 4.8 all-to-all-start.5
  409.3 16.6 %all-to-all-done.5 = f32[16,32,1024]{2,0,1:T(8,128)} async-done(((f32[16,32,1024]{2,0,1:T(8,128)}), f32[16,32,1024]{2,0,1:T(8,128)}, u32[]{:S(2)}, u32[]{:S(2)}) %all-to-all-start.5) | async-done | bytes 2097184 | tf_op jit(solution)/shard_map/all_to_all | solution.py:101
  429.6 17.6 %multiply_reduce_fusion.11 = (f32[]{:T(128)}, f32[]{:T(128)}, f32[32,16,1024]{2,1,0:T(8,128)}) fusion(f32[32,16,1024]{2,1,0:T(8,128)S(1)} %get-tuple-element.257, f32[]{:T(128)S(6)} %sqrt.15, f32[32,16,1024]{2,1,0:T(8,128)S(1)} %copy-done.3, f32[32,16,1024]{2,0,1:T(8,128)S(1)} %fusion.134, f32[1792,1024]{1,0:T(8,128)} %fusion.10, ...), kind=kOutput, calls=%fused_computation.107 | convolution fusion | flops 11280842752 | bytes 17307660 | tf_op jit(solution)/shard_map/dot_general | solution.py:63
  448.6 38.6 %psum.66 = f32[2]{0:T(128)S(1)} all-reduce(f32[2]{0:T(128)S(1)} %pad_maximum_fusion), channel_id=1, replica_groups=mesh['node'=16,'tone'=2] {'node','tone'}, use_global_device_ids=true, to_apply=%region_9.10 | all-reduce | flops 2 | bytes 16 | tf_op jit(solution)/shard_map/psum | solution.py:119
  487.8 6.2 multiply_reduce_fusion.9
  494.1 40.7 %psum.67 = f32[]{:T(128)} all-reduce(f32[]{:T(128)} %get-tuple-element.193), channel_id=1, replica_groups=mesh['node'=16,'tone'=2] {'node','tone'}, use_global_device_ids=true, to_apply=%region_11.12 | all-reduce | flops 1 | bytes 8 | tf_op jit(solution)/shard_map/psum | solution.py:122
  541.5 27.1 %all_to_all.181 = f32[32,16,1024]{2,1,0:T(8,128)S(1)} all-to-all(f32[32,16,1024]{2,1,0:T(8,128)S(1)} %copy.131), channel_id=1, replica_groups=mesh['node'=16,'tone'=2] {'tone'}, dimensions={0} | all-to-all | bytes 4194304 | tf_op jit(solution)/shard_map/all_to_all | solution.py:95
  576.2 4.8 all-to-all-start.7
  587.1 16.7 %all-to-all-done.7 = f32[16,32,1024]{2,0,1:T(8,128)} async-done(((f32[16,32,1024]{2,0,1:T(8,128)}), f32[16,32,1024]{2,0,1:T(8,128)}, u32[]{:S(2)}, u32[]{:S(2)}) %all-to-all-start.7) | async-done | bytes 2097184 | tf_op jit(solution)/shard_map/all_to_all | solution.py:101
  607.7 17.6 %multiply_reduce_fusion.8 = (f32[]{:T(128)}, f32[]{:T(128)}, f32[]{:T(128)}, f32[32,16,1024]{2,1,0:T(8,128)}) fusion(f32[32,16,1024]{2,1,0:T(8,128)S(1)} %get-tuple-element.257, f32[]{:T(128)S(6)} %sqrt.15, f32[32,16,1024]{2,1,0:T(8,128)S(1)} %copy-done.23, f32[32,16,1024]{2,1,0:T(8,128)S(1)} %copy-done.4, f32[32,16,1024]{2,0,1:T(8,128)S(1)} %fusion.128, ...), kind=kOutput, calls=%fused_computation.103 | convolution fusion | flops 11281891328 | bytes 19404816 | tf_op jit(solution)/shard_map/dot_general | solution.py:63
  627.3 38.9 %psum.68 = f32[3]{0:T(128)S(1)} all-reduce(f32[3]{0:T(128)S(1)} %pad_maximum_fusion.1), channel_id=1, replica_groups=mesh['node'=16,'tone'=2] {'node','tone'}, use_global_device_ids=true, to_apply=%region_16.17 | all-reduce | flops 3 | bytes 24 | tf_op jit(solution)/shard_map/psum | solution.py:119
  666.8 7.7 multiply_reduce_fusion.5
  674.5 41.0 %psum.69 = f32[]{:T(128)} all-reduce(f32[]{:T(128)} %get-tuple-element.191), channel_id=1, replica_groups=mesh['node'=16,'tone'=2] {'node','tone'}, use_global_device_ids=true, to_apply=%region_18.19 | all-reduce | flops 1 | bytes 8 | tf_op jit(solution)/shard_map/psum | solution.py:122
  723.6 5.0 all-to-all-start.8
  730.6 22.6 %all-to-all-done.8 = f32[32,16,1024]{2,1,0:T(8,128)} async-done(((f32[32,16,1024]{2,1,0:T(8,128)}), f32[32,16,1024]{2,1,0:T(8,128)}, u32[]{:S(2)}, u32[]{:S(2)}) %all-to-all-start.8) | async-done | bytes 2097184 | tf_op jit(solution)/shard_map/all_to_all | solution.py:95
  762.3 5.0 all-to-all-start.9
  781.5 9.0 all-to-all-done.9
  794.9 18.1 %multiply_reduce_fusion.4 = (f32[]{:T(128)}, f32[]{:T(128)}, f32[]{:T(128)}, f32[]{:T(128)}, f32[32,16,1024]{2,1,0:T(8,128)}) fusion(f32[32,16,1024]{2,1,0:T(8,128)S(1)} %get-tuple-element.257, f32[]{:T(128)S(6)} %sqrt.15, f32[32,16,1024]{2,1,0:T(8,128)S(1)} %copy-done.13, f32[]{:T(128)} %sqrt.18, f32[32,16,1024]{2,1,0:T(8,128)S(1)} %copy-done.24, ...), kind=kOutput, calls=%fused_computation.98 | convolution fusion | flops 11283464192 | bytes 23599128 | tf_op jit(solution)/shard_map/dot_general | solution.py:63
  817.0 38.6 %psum.70 = f32[4]{0:T(128)S(1)} all-reduce(f32[4]{0:T(128)S(1)} %pad_maximum_fusion.2), channel_id=1, replica_groups=mesh['node'=16,'tone'=2] {'node','tone'}, use_global_device_ids=true, to_apply=%region_24.25 | all-reduce | flops 4 | bytes 32 | tf_op jit(solution)/shard_map/psum | solution.py:119
  856.3 7.6 multiply_reduce_fusion
  864.0 39.6 %psum.71 = f32[]{:T(128)} all-reduce(f32[]{:T(128)} %multiply_reduce_fusion), channel_id=1, replica_groups=mesh['node'=16,'tone'=2] {'node','tone'}, use_global_device_ids=true, to_apply=%region_26.27 | all-reduce | flops 1 | bytes 8 | tf_op jit(solution)/shard_map/psum | solution.py:122
  926.7 6.5 add_add_fusion
  934.1 8.2 multiply_subtract_fusion
  (198 shorter events, 157.1 us)
Async XLA Ops:
  0.6 46.0 %copy-start = (f32[3,4]{1,0:T(4,128)S(1)}, f32[3,4]{1,0:T(4,128)}, u32[]{:S(2)}) copy-start(f32[3,4]{1,0:T(4,128)} %param.47) | copy-start | bytes 148
  7.8 5.0 copy-start.15
  7.8 68.8 %all-to-all-start = ((f32[32,16,1024]{2,1,0:T(8,128)}), f32[32,16,1024]{2,1,0:T(8,128)}, u32[]{:S(2)}, u32[]{:S(2)}) async-start(f32[32,16,1024]{2,1,0:T(8,128)} %copy.113), calls=%async_computation | async-start | bytes 4194304 | tf_op jit(solution)/shard_map/all_to_all | solution.py:95
  12.8 6.2 copy-start.32
  14.1 103.0 %collective-permute-start = (f32[32,16,384]{2,1,0:T(8,128)}, f32[32,16,384]{2,1,0:T(8,128)}, u32[]{:S(2)}, u32[]{:S(2)}) collective-permute-start(f32[32,16,384]{2,1,0:T(8,128)} %get-tuple-element.210), channel_id=1, source_target_pairs={{0,2},{2,4},{4,6},{6,8},{8,10},{10,12},{12,14},{14,16},{16,18},{18... | collective-permute-start | bytes 2359304 | tf_op jit(solution)/shard_map/ppermute | solution.py:24
  17.4 99.7 %collective-permute-start.1 = (f32[32,16,384]{2,1,0:T(8,128)}, f32[32,16,384]{2,1,0:T(8,128)}, u32[]{:S(2)}, u32[]{:S(2)}) collective-permute-start(f32[32,16,384]{2,1,0:T(8,128)} %get-tuple-element.211), channel_id=1, source_target_pairs={{2,0},{4,2},{6,4},{8,6},{10,8},{12,10},{14,12},{16,14},{18,16},{20... | collective-permute-start | bytes 2359304 | tf_op jit(solution)/shard_map/ppermute | solution.py:25
  19.0 2.4 copy-start.35
  43.6 3.0 copy-start.33
  43.6 3.1 copy-start.31
  46.8 6.3 copy-start.21
  53.2 5.8 copy-start.20
  59.0 5.9 copy-start.19
  64.9 5.9 copy-start.18
  80.4 3.1 copy-start.7
  86.0 28.9 %all-to-all-start.1 = ((f32[16,32,1024]{2,0,1:T(8,128)}), f32[16,32,1024]{2,0,1:T(8,128)S(1)}, u32[]{:S(2)}, u32[]{:S(2)}) async-start(f32[16,32,1024]{2,0,1:T(8,128)} %copy.115), calls=%async_computation.1 | async-start | bytes 4194304 | tf_op jit(solution)/shard_map/all_to_all | solution.py:101
  89.8 7.2 copy-start.17
  115.1 2.2 copy-start.30
  177.6 3.0 copy-start.27
  183.2 30.2 %all-to-all-start.2 = ((f32[32,16,1024]{2,1,0:T(8,128)}), f32[32,16,1024]{2,1,0:T(8,128)}, u32[]{:S(2)}, u32[]{:S(2)}) async-start(f32[32,16,1024]{2,1,0:T(8,128)} %copy.119), calls=%async_computation.2 | async-start | bytes 4194304 | tf_op jit(solution)/shard_map/all_to_all | solution.py:95
  222.5 28.6 %all-to-all-start.3 = ((f32[16,32,1024]{2,0,1:T(8,128)}), f32[16,32,1024]{2,0,1:T(8,128)}, u32[]{:S(2)}, u32[]{:S(2)}) async-start(f32[16,32,1024]{2,0,1:T(8,128)} %copy.121), calls=%async_computation.3 | async-start | bytes 4194304 | tf_op jit(solution)/shard_map/all_to_all | solution.py:101
  229.7 25.1 %collective-permute-start.2 = (f32[32,16,384]{2,1,0:T(8,128)}, f32[32,16,384]{2,1,0:T(8,128)}, u32[]{:S(2)}, u32[]{:S(2)}) collective-permute-start(f32[32,16,384]{2,1,0:T(8,128)} %get-tuple-element.208), channel_id=1, source_target_pairs={{0,2},{2,4},{4,6},{6,8},{8,10},{10,12},{12,14},{14,16},{16,18},{18... | collective-permute-start | bytes 2359304 | tf_op jit(solution)/shard_map/ppermute | solution.py:24
  231.9 22.9 %collective-permute-start.3 = (f32[32,16,384]{2,1,0:T(8,128)S(1)}, f32[32,16,384]{2,1,0:T(8,128)}, u32[]{:S(2)}, u32[]{:S(2)}) collective-permute-start(f32[32,16,384]{2,1,0:T(8,128)S(1)} %get-tuple-element.209), channel_id=1, source_target_pairs={{2,0},{4,2},{6,4},{8,6},{10,8},{12,10},{14,12},{16,14},{18,16},{20... | collective-permute-start | bytes 2359304 | tf_op jit(solution)/shard_map/ppermute | solution.py:25
  359.3 3.1 copy-start.2
  391.0 2.1 copy-start.9
  398.4 27.6 %all-to-all-start.5 = ((f32[16,32,1024]{2,0,1:T(8,128)}), f32[16,32,1024]{2,0,1:T(8,128)}, u32[]{:S(2)}, u32[]{:S(2)}) async-start(f32[16,32,1024]{2,0,1:T(8,128)} %copy.127), calls=%async_computation.5 | async-start | bytes 4194304 | tf_op jit(solution)/shard_map/all_to_all | solution.py:101
  405.6 24.0 %collective-permute-start.4 = (f32[32,16,384]{2,1,0:T(8,128)}, f32[32,16,384]{2,1,0:T(8,128)}, u32[]{:S(2)}, u32[]{:S(2)}) collective-permute-start(f32[32,16,384]{2,1,0:T(8,128)} %get-tuple-element.206), channel_id=1, source_target_pairs={{0,2},{2,4},{4,6},{6,8},{8,10},{10,12},{12,14},{14,16},{16,18},{18... | collective-permute-start | bytes 2359304 | tf_op jit(solution)/shard_map/ppermute | solution.py:24
  407.8 21.8 %collective-permute-start.5 = (f32[32,16,384]{2,1,0:T(8,128)S(1)}, f32[32,16,384]{2,1,0:T(8,128)}, u32[]{:S(2)}, u32[]{:S(2)}) collective-permute-start(f32[32,16,384]{2,1,0:T(8,128)S(1)} %get-tuple-element.207), channel_id=1, source_target_pairs={{2,0},{4,2},{6,4},{8,6},{10,8},{12,10},{14,12},{16,14},{18,16},{20... | collective-permute-start | bytes 2359304 | tf_op jit(solution)/shard_map/ppermute | solution.py:25
  537.2 3.1 copy-start.22
  568.9 2.1 copy-start.10
  576.2 27.5 %all-to-all-start.7 = ((f32[16,32,1024]{2,0,1:T(8,128)}), f32[16,32,1024]{2,0,1:T(8,128)}, u32[]{:S(2)}, u32[]{:S(2)}) async-start(f32[16,32,1024]{2,0,1:T(8,128)} %copy.133), calls=%async_computation.7 | async-start | bytes 4194304 | tf_op jit(solution)/shard_map/all_to_all | solution.py:101
  583.4 24.0 %collective-permute-start.6 = (f32[32,16,384]{2,1,0:T(8,128)}, f32[32,16,384]{2,1,0:T(8,128)}, u32[]{:S(2)}, u32[]{:S(2)}) collective-permute-start(f32[32,16,384]{2,1,0:T(8,128)} %get-tuple-element.204), channel_id=1, source_target_pairs={{0,2},{2,4},{4,6},{6,8},{8,10},{10,12},{12,14},{14,16},{16,18},{18... | collective-permute-start | bytes 2359304 | tf_op jit(solution)/shard_map/ppermute | solution.py:24
  585.6 21.9 %collective-permute-start.7 = (f32[32,16,384]{2,1,0:T(8,128)S(1)}, f32[32,16,384]{2,1,0:T(8,128)}, u32[]{:S(2)}, u32[]{:S(2)}) collective-permute-start(f32[32,16,384]{2,1,0:T(8,128)S(1)} %get-tuple-element.205), channel_id=1, source_target_pairs={{2,0},{4,2},{6,4},{8,6},{10,8},{12,10},{14,12},{16,14},{18,16},{20... | collective-permute-start | bytes 2359304 | tf_op jit(solution)/shard_map/ppermute | solution.py:25
  605.5 2.2 copy-start.23
  718.0 3.0 copy-start.25
  723.6 6.3 copy-start.37
  723.6 29.5 %all-to-all-start.8 = ((f32[32,16,1024]{2,1,0:T(8,128)}), f32[32,16,1024]{2,1,0:T(8,128)}, u32[]{:S(2)}, u32[]{:S(2)}) async-start(f32[32,16,1024]{2,1,0:T(8,128)} %copy.137), calls=%async_computation.8 | async-start | bytes 4194304 | tf_op jit(solution)/shard_map/all_to_all | solution.py:95
  762.3 5.0 copy-start.36
  762.3 28.2 %all-to-all-start.9 = ((f32[16,32,1024]{2,0,1:T(8,128)}), f32[16,32,1024]{2,0,1:T(8,128)}, u32[]{:S(2)}, u32[]{:S(2)}) async-start(f32[16,32,1024]{2,0,1:T(8,128)} %copy.139), calls=%async_computation.9 | async-start | bytes 4194304 | tf_op jit(solution)/shard_map/all_to_all | solution.py:101
  770.4 24.0 %collective-permute-start.8 = (f32[32,16,384]{2,1,0:T(8,128)}, f32[32,16,384]{2,1,0:T(8,128)}, u32[]{:S(2)}, u32[]{:S(2)}) collective-permute-start(f32[32,16,384]{2,1,0:T(8,128)} %get-tuple-element.202), channel_id=1, source_target_pairs={{0,2},{2,4},{4,6},{6,8},{8,10},{10,12},{12,14},{14,16},{16,18},{18... | collective-permute-start | bytes 2359304 | tf_op jit(solution)/shard_map/ppermute | solution.py:24
  772.5 21.9 %collective-permute-start.9 = (f32[32,16,384]{2,1,0:T(8,128)S(1)}, f32[32,16,384]{2,1,0:T(8,128)}, u32[]{:S(2)}, u32[]{:S(2)}) collective-permute-start(f32[32,16,384]{2,1,0:T(8,128)S(1)} %get-tuple-element.203), channel_id=1, source_target_pairs={{2,0},{4,2},{6,4},{8,6},{10,8},{12,10},{14,12},{16,14},{18,16},{20... | collective-permute-start | bytes 2359304 | tf_op jit(solution)/shard_map/ppermute | solution.py:25
  790.5 3.9 copy-start.24
  790.5 3.9 copy-start.26
  792.4 2.4 copy-start.13
  926.7 7.4 copy-start.6
  926.7 7.4 copy-start.12
  926.7 7.4 copy-start.14
  926.7 7.4 copy-start.29
  934.1 8.2 copy-start.1
  (8 other events, 16.4 us)
where the time goes:
time: 949 us; the launch traced here: 942 us
  blocking collectives  414 us (44%)
  matrix products  143 us (15%)
  waiting for transfers between devices  120 us (13%)
  other arithmetic  110 us (12%)
  local copies, waits for them, and re-layouts  77 us (8%)
  starting transfers between devices  57.6 us (6%)
  between operations  20.7 us (2%)
    psum x4, blocking collectives, per_device(): length = jnp.sqrt(lax.psum(jnp.sum(image * image), ('node', 'tone')))  163 us
    psum x4, blocking collectives, per_device(): projected = lax.psum(local_terms, ('node', 'tone'))  155 us
    dot_general x5, matrix products, couple(): jnp.dot(padded.reshape(rows, padded.shape[2]), operator, precision=HIGH)  87.9 us
    all_to_all x5, waiting for transfers between devices, to_freq(): lax.all_to_all(along_second(second, field), 'tone', split_axis=1, concat_...  72.1 us
    all_to_all x2, blocking collectives, to_time(): lax.all_to_all(along_first(first, field), 'tone', split_axis=0, concat_ax...  54.2 us
    all_to_all x3, waiting for transfers between devices, to_time(): lax.all_to_all(along_first(first, field), 'tone', split_axis=0, concat_ax...  47.7 us
    psum x1, blocking collectives, per_device(): beta = jnp.sqrt(lax.psum(jnp.sum(start * start), ('node', 'tone')))  42.4 us
    scatter-add x6, other arithmetic, band_matrix(): operator = operator.at[offset * NB:offset * NB + nodes].add(placed)  36.2 us
  transfers between devices with their start and end apart: 18, of which 7 were waited for; matrix products, arithmetic and copies ran while one was open for 13% of the time, Pallas kernels for 0%

commit v1 on v0

--- a/solution.py
+++ b/solution.py
@@ -12,6 +12,10 @@
 M = 4
 NTYPES = 4
 HIGH = lax.Precision.HIGHEST
+place_files = lambda t0, out_dim, dim_no: jnp.concatenate(
+    lax.all_to_all(jnp.stack(jnp.split(t0, lax.psum(1, "tone"), axis=out_dim)), "tone", 0, 0),
+    axis=dim_no,
+)
 
 
 def extended(value, sides, width):
@@ -98,9 +102,7 @@
         return along_second(second, moved)
 
     def to_freq(field):
-        moved = lax.all_to_all(
-            along_second(second, field), "tone", split_axis=1, concat_axis=0, tiled=True
-        )
+        moved = place_files(along_second(second, field), 1, 0)
         return along_first(first, moved)
 
     linear, amplitude, sharpness = (per_node[0], per_node[1], per_node[2])

time: 949 us -> 951 us (level)
  local copies, waits for them, and re-layouts: 77 us -> 58.3 us
  matrix products: 143 us -> 157 us
    transpose x5 -> x0, local copies, waits for them, and re-layouts: 12.7 us -> none  [along_second(): return jnp.einsum('sq,tqn->tsn', table, field, precision=HIGH)]
    dot_general x10, matrix products: 26.4 us -> 38.7 us  [along_first(): return jnp.einsum('tk,kqn->tqn', table, field, precision=HIGH)]
where the time goes in v1:
time: 951 us; the launch traced here: 945 us
  blocking collectives  414 us (44%)
  matrix products  157 us (17%)
  waiting for transfers between devices  120 us (13%)
  other arithmetic  117 us (12%)
  local copies, waits for them, and re-layouts  58.3 us (6%)
  starting transfers between devices  57.3 us (6%)
  between operations  20.5 us (2%)
    psum x4, blocking collectives, per_device(): length = jnp.sqrt(lax.psum(jnp.sum(image * image), ('node', 'tone')))  163 us
    psum x4, blocking collectives, per_device(): projected = lax.psum(local_terms, ('node', 'tone'))  155 us
    dot_general x5, matrix products, couple(): jnp.dot(padded.reshape(rows, padded.shape[2]), operator, precision=HIGH)  89.3 us
    all_to_all x5, waiting for transfers between devices, lax.all_to_all(jnp.stack(jnp.split(t0, lax.psum(1, 'tone'), axis=out_dim)...  72.5 us
    all_to_all x2, blocking collectives, to_time(): lax.all_to_all(along_first(first, field), 'tone', split_axis=0, concat_ax...  54.1 us
    all_to_all x3, waiting for transfers between devices, to_time(): lax.all_to_all(along_first(first, field), 'tone', split_axis=0, concat_ax...  47.9 us
    psum x1, blocking collectives, per_device(): beta = jnp.sqrt(lax.psum(jnp.sum(start * start), ('node', 'tone')))  42.5 us
    dot_general x10, matrix products, along_first(): return jnp.einsum('tk,kqn->tqn', table, field, precision=HIGH)  38.7 us
  transfers between devices with their start and end apart: 18, of which 7 were waited for; matrix products, arithmetic and copies ran while one was open for 13% of the time, Pallas kernels for 0%

profile of v1, /device:TPU:0, one launch (start us, length us, event | category | flops | bytes accessed | tf_op | source)
XLA Modules:
  0.0 944.5 jit_solution(297518831957517880)
XLA Ops:
  0.6 4.6 fusion.82
  7.8 5.0 all-to-all-start
  33.9 9.7 %broadcast_multiply_fusion = (f32[8,8,128,128]{2,1,3,0:T(8,128)}, f32[8,8,128,128]{2,1,3,0:T(8,128)}, f32[8,8,128,128]{2,1,3,0:T(8,128)}, f32[8,8,128,128]{2,1,3...) fusion(f32[8,128,128]{1,2,0:T(8,128)} %copy.106, ...), kind=kLoop, calls=%fused_computation.131 | loop fusion | flops 7340032 | bytes 33030400 | tf_op jit(solution)/shard_map/bsc,bd->bcds/dot_general | solution.py:58
  46.9 6.3 scatter-add.24
  53.2 5.8 fusion.15
  59.1 5.9 fusion.14
  64.9 5.9 fusion.13
  70.9 5.7 fusion.12
  90.5 7.2 fusion.11
  97.7 5.7 fusion.10
  103.4 12.2 %all-to-all-done.1 = f32[2,16,16,1024]{3,2,1,0:T(8,128)S(1)} async-done(((f32[2,16,16,1024]{3,2,1,0:T(8,128)}), f32[2,16,16,1024]{3,2,1,0:T(8,128)S(1)}, u32[]{:S(2)}, u32[]{:S(2)}) %all-to-all-start.1) | async-done | bytes 2097184 | tf_op jit(solution)/shard_map/all_to_all | solution.py:16
  118.7 17.1 %multiply_reduce_fusion.14 = (f32[]{:T(128)}, f32[32,16,1024]{2,1,0:T(8,128)S(1)}) fusion(f32[32,16,1024]{2,0,1:T(8,128)S(1)} %fusion.80, f32[32,16,1024]{2,1,0:T(8,128)S(1)} %copy-done.28, f32[1792,1024]{1,0:T(8,128)} %fusion.10, f32[32,16,384]{2,1,0:T(8,128)} %collective-permute-done.1, f32[32,16,1024]{2,1,0:T(8,128)S(1)} %copy-done.16, ...), kind=kOutput, calls=%fused_computation.126 | convolution fusion | flops 11279794176 | bytes 17307652 | tf_op jit(solution)/shard_map/dot_general | solution.py:67
  135.8 42.5 %psum.63 = f32[]{:T(128)} all-reduce(f32[]{:T(128)} %get-tuple-element.266), channel_id=1, replica_groups=mesh['node'=16,'tone'=2] {'node','tone'}, use_global_device_ids=true, to_apply=%region_1.2 | all-reduce | flops 1 | bytes 8 | tf_op jit(solution)/shard_map/psum | solution.py:114
  184.8 5.2 all-to-all-start.2
  190.0 25.2 %all-to-all-done.2 = f32[32,16,1024]{2,1,0:T(8,128)} async-done(((f32[32,16,1024]{2,1,0:T(8,128)}), f32[32,16,1024]{2,1,0:T(8,128)}, u32[]{:S(2)}, u32[]{:S(2)}) %all-to-all-start.2) | async-done | bytes 2097184 | tf_op jit(solution)/shard_map/all_to_all | solution.py:99
  223.5 4.8 all-to-all-start.3
  234.1 18.0 %all-to-all-done.3 = f32[2,16,16,1024]{3,2,1,0:T(8,128)} async-done(((f32[2,16,16,1024]{3,2,1,0:T(8,128)}), f32[2,16,16,1024]{3,2,1,0:T(8,128)}, u32[]{:S(2)}, u32[]{:S(2)}) %all-to-all-start.3) | async-done | bytes 2097184 | tf_op jit(solution)/shard_map/all_to_all | solution.py:16
  252.1 4.7 fusion.76
  256.9 17.4 %multiply_reduce_fusion.13 = (f32[]{:T(128)}, f32[32,16,1024]{2,1,0:T(8,128)}) fusion(f32[32,16,1024]{2,1,0:T(8,128)S(1)} %get-tuple-element.267, f32[]{:T(128)S(6)} %sqrt.15, f32[32,16,1024]{2,0,1:T(8,128)S(1)} %fusion.76, f32[1792,1024]{1,0:T(8,128)} %fusion.10, f32[32,16,384]{2,1,0:T(8,128)} %collective-permute-done.3, ...), kind=kOutput, calls=%fused_computation.125 | convolution fusion | flops 11279794176 | bytes 17307656 | tf_op jit(solution)/shard_map/dot_general | solution.py:67
  274.3 38.9 %psum.64 = f32[1]{0:T(128)} all-reduce(f32[1]{0:T(128)} %bitcast.38), channel_id=1, replica_groups=mesh['node'=16,'tone'=2] {'node','tone'}, use_global_device_ids=true, to_apply=%region_3.4 | all-reduce | flops 1 | bytes 8 | tf_op jit(solution)/shard_map/psum | solution.py:121
  316.5 41.1 %psum.65 = f32[]{:T(128)} all-reduce(f32[]{:T(128)} %multiply_reduce_fusion.12), channel_id=1, replica_groups=mesh['node'=16,'tone'=2] {'node','tone'}, use_global_device_ids=true, to_apply=%region_5.6 | all-reduce | flops 1 | bytes 8 | tf_op jit(solution)/shard_map/psum | solution.py:124
  365.2 27.0 %all_to_all.115 = f32[32,16,1024]{2,1,0:T(8,128)S(1)} all-to-all(f32[32,16,1024]{2,1,0:T(8,128)S(1)} %copy.118), channel_id=1, replica_groups=mesh['node'=16,'tone'=2] {'tone'}, dimensions={0} | all-to-all | bytes 4194304 | tf_op jit(solution)/shard_map/all_to_all | solution.py:99
  399.0 4.8 all-to-all-start.5
  409.9 16.6 %all-to-all-done.5 = f32[2,16,16,1024]{3,2,1,0:T(8,128)} async-done(((f32[2,16,16,1024]{3,2,1,0:T(8,128)}), f32[2,16,16,1024]{3,2,1,0:T(8,128)}, u32[]{:S(2)}, u32[]{:S(2)}) %all-to-all-start.5) | async-done | bytes 2097184 | tf_op jit(solution)/shard_map/all_to_all | solution.py:16
  426.5 4.7 fusion.72
  431.3 17.6 %multiply_reduce_fusion.11 = (f32[]{:T(128)}, f32[]{:T(128)}, f32[32,16,1024]{2,1,0:T(8,128)}) fusion(f32[32,16,1024]{2,1,0:T(8,128)S(1)} %get-tuple-element.267, f32[]{:T(128)S(6)} %sqrt.15, f32[32,16,1024]{2,1,0:T(8,128)S(1)} %copy-done.3, f32[32,16,1024]{2,0,1:T(8,128)S(1)} %fusion.72, f32[1792,1024]{1,0:T(8,128)} %fusion.10, ...), kind=kOutput, calls=%fused_computation.122 | convolution fusion | flops 11280842752 | bytes 17307660 | tf_op jit(solution)/shard_map/dot_general | solution.py:67
  450.2 38.6 %psum.66 = f32[2]{0:T(128)S(1)} all-reduce(f32[2]{0:T(128)S(1)} %pad_maximum_fusion.5), channel_id=1, replica_groups=mesh['node'=16,'tone'=2] {'node','tone'}, use_global_device_ids=true, to_apply=%region_9.10 | all-reduce | flops 2 | bytes 16 | tf_op jit(solution)/shard_map/psum | solution.py:121
  489.4 6.1 multiply_reduce_fusion.9
  495.5 40.7 %psum.67 = f32[]{:T(128)} all-reduce(f32[]{:T(128)} %get-tuple-element.193), channel_id=1, replica_groups=mesh['node'=16,'tone'=2] {'node','tone'}, use_global_device_ids=true, to_apply=%region_11.12 | all-reduce | flops 1 | bytes 8 | tf_op jit(solution)/shard_map/psum | solution.py:124
  542.9 27.0 %all_to_all.116 = f32[32,16,1024]{2,1,0:T(8,128)S(1)} all-to-all(f32[32,16,1024]{2,1,0:T(8,128)S(1)} %copy.123), channel_id=1, replica_groups=mesh['node'=16,'tone'=2] {'tone'}, dimensions={0} | all-to-all | bytes 4194304 | tf_op jit(solution)/shard_map/all_to_all | solution.py:99
  576.7 4.8 all-to-all-start.7
  587.5 16.7 %all-to-all-done.7 = f32[2,16,16,1024]{3,2,1,0:T(8,128)} async-done(((f32[2,16,16,1024]{3,2,1,0:T(8,128)}), f32[2,16,16,1024]{3,2,1,0:T(8,128)}, u32[]{:S(2)}, u32[]{:S(2)}) %all-to-all-start.7) | async-done | bytes 2097184 | tf_op jit(solution)/shard_map/all_to_all | solution.py:16
  604.2 4.7 fusion.68
  609.0 17.6 %multiply_reduce_fusion.8 = (f32[]{:T(128)}, f32[]{:T(128)}, f32[]{:T(128)}, f32[32,16,1024]{2,1,0:T(8,128)}) fusion(f32[32,16,1024]{2,1,0:T(8,128)S(1)} %get-tuple-element.267, f32[]{:T(128)S(6)} %sqrt.15, f32[32,16,1024]{2,1,0:T(8,128)S(1)} %copy-done.23, f32[32,16,1024]{2,1,0:T(8,128)S(1)} %copy-done.4, f32[32,16,1024]{2,0,1:T(8,128)S(1)} %fusion.68, ...), kind=kOutput, calls=%fused_computation.118 | convolution fusion | flops 11281891328 | bytes 19404816 | tf_op jit(solution)/shard_map/dot_general | solution.py:67
  628.6 38.9 %psum.68 = f32[3]{0:T(128)S(1)} all-reduce(f32[3]{0:T(128)S(1)} %pad_maximum_fusion.6), channel_id=1, replica_groups=mesh['node'=16,'tone'=2] {'node','tone'}, use_global_device_ids=true, to_apply=%region_16.17 | all-reduce | flops 3 | bytes 24 | tf_op jit(solution)/shard_map/psum | solution.py:121
  668.2 7.8 multiply_reduce_fusion.5
  675.9 41.1 %psum.69 = f32[]{:T(128)} all-reduce(f32[]{:T(128)} %get-tuple-element.191), channel_id=1, replica_groups=mesh['node'=16,'tone'=2] {'node','tone'}, use_global_device_ids=true, to_apply=%region_18.19 | all-reduce | flops 1 | bytes 8 | tf_op jit(solution)/shard_map/psum | solution.py:124
  725.2 4.9 all-to-all-start.8
  732.0 22.8 %all-to-all-done.8 = f32[32,16,1024]{2,1,0:T(8,128)} async-done(((f32[32,16,1024]{2,1,0:T(8,128)}), f32[32,16,1024]{2,1,0:T(8,128)}, u32[]{:S(2)}, u32[]{:S(2)}) %all-to-all-start.8) | async-done | bytes 2097184 | tf_op jit(solution)/shard_map/all_to_all | solution.py:99
  763.0 4.9 all-to-all-start.9
  782.3 9.0 all-to-all-done.9
  791.2 4.7 fusion.64
  796.0 19.5 %multiply_reduce_fusion.4 = (f32[]{:T(128)}, f32[]{:T(128)}, f32[]{:T(128)}, f32[]{:T(128)}, f32[32,16,1024]{2,1,0:T(8,128)}) fusion(f32[32,16,1024]{2,1,0:T(8,128)S(1)} %get-tuple-element.267, f32[]{:T(128)S(6)} %sqrt.15, f32[32,16,1024]{2,1,0:T(8,128)S(1)} %copy-done.13, f32[]{:T(128)} %sqrt.18, f32[32,16,1024]{2,1,0:T(8,128)} %copy-done.22, ...), kind=kOutput, calls=%fused_computation.113 | convolution fusion | flops 11283464192 | bytes 23599128 | tf_op jit(solution)/shard_map/dot_general | solution.py:67
  819.7 38.7 %psum.70 = f32[4]{0:T(128)S(1)} all-reduce(f32[4]{0:T(128)S(1)} %pad_maximum_fusion.7), channel_id=1, replica_groups=mesh['node'=16,'tone'=2] {'node','tone'}, use_global_device_ids=true, to_apply=%region_24.25 | all-reduce | flops 4 | bytes 32 | tf_op jit(solution)/shard_map/psum | solution.py:121
  859.0 7.5 multiply_reduce_fusion
  866.6 40.0 %psum.71 = f32[]{:T(128)} all-reduce(f32[]{:T(128)} %multiply_reduce_fusion), channel_id=1, replica_groups=mesh['node'=16,'tone'=2] {'node','tone'}, use_global_device_ids=true, to_apply=%region_26.27 | all-reduce | flops 1 | bytes 8 | tf_op jit(solution)/shard_map/psum | solution.py:124
  929.1 6.3 add_add_fusion
  936.3 8.0 multiply_subtract_fusion
  (194 shorter events, 154.1 us)
Async XLA Ops:
  0.6 46.0 %copy-start = (f32[3,4]{1,0:T(4,128)S(1)}, f32[3,4]{1,0:T(4,128)}, u32[]{:S(2)}) copy-start(f32[3,4]{1,0:T(4,128)} %param.47) | copy-start | bytes 148
  7.8 5.0 copy-start.15
  7.8 68.8 %all-to-all-start = ((f32[32,16,1024]{2,1,0:T(8,128)}), f32[32,16,1024]{2,1,0:T(8,128)}, u32[]{:S(2)}, u32[]{:S(2)}) async-start(f32[32,16,1024]{2,1,0:T(8,128)} %copy.108), calls=%async_computation | async-start | bytes 4194304 | tf_op jit(solution)/shard_map/all_to_all | solution.py:99
  12.8 6.2 copy-start.30
  14.1 104.6 %collective-permute-start = (f32[32,16,384]{2,1,0:T(8,128)}, f32[32,16,384]{2,1,0:T(8,128)}, u32[]{:S(2)}, u32[]{:S(2)}) collective-permute-start(f32[32,16,384]{2,1,0:T(8,128)} %get-tuple-element.218), channel_id=1, source_target_pairs={{0,2},{2,4},{4,6},{6,8},{8,10},{10,12},{12,14},{14,16},{16,18},{18... | collective-permute-start | bytes 2359304 | tf_op jit(solution)/shard_map/ppermute | solution.py:28
  17.4 101.3 %collective-permute-start.1 = (f32[32,16,384]{2,1,0:T(8,128)}, f32[32,16,384]{2,1,0:T(8,128)}, u32[]{:S(2)}, u32[]{:S(2)}) collective-permute-start(f32[32,16,384]{2,1,0:T(8,128)} %get-tuple-element.219), channel_id=1, source_target_pairs={{2,0},{4,2},{6,4},{8,6},{10,8},{12,10},{14,12},{16,14},{18,16},{20... | collective-permute-start | bytes 2359304 | tf_op jit(solution)/shard_map/ppermute | solution.py:29
  43.7 3.0 copy-start.31
  43.7 3.1 copy-start.29
  46.9 6.3 copy-start.21
  53.2 5.9 copy-start.20
  59.1 5.9 copy-start.19
  64.9 5.9 copy-start.18
  86.7 28.9 %all-to-all-start.1 = ((f32[2,16,16,1024]{3,2,1,0:T(8,128)}), f32[2,16,16,1024]{3,2,1,0:T(8,128)S(1)}, u32[]{:S(2)}, u32[]{:S(2)}) async-start(f32[2,16,16,1024]{3,2,1,0:T(8,128)} %pad_maximum_fusion), calls=%async_computation.1 | async-start | bytes 4194304 | tf_op jit(solution)/shard_map/all_to_all | solution.py:16
  90.5 7.2 copy-start.17
  97.7 21.0 %copy-start.32 = (f32[1024]{0:T(1024)S(1)}, f32[1024]{0:T(1024)}, u32[]{:S(2)}) copy-start(f32[1024]{0:T(1024)} %param.44) | copy-start | bytes 12292
  115.6 3.1 copy-start.16
  115.6 3.1 copy-start.28
  179.2 3.1 copy-start.25
  184.8 30.4 %all-to-all-start.2 = ((f32[32,16,1024]{2,1,0:T(8,128)}), f32[32,16,1024]{2,1,0:T(8,128)}, u32[]{:S(2)}, u32[]{:S(2)}) async-start(f32[32,16,1024]{2,1,0:T(8,128)} %copy.113), calls=%async_computation.2 | async-start | bytes 4194304 | tf_op jit(solution)/shard_map/all_to_all | solution.py:99
  223.5 28.6 %all-to-all-start.3 = ((f32[2,16,16,1024]{3,2,1,0:T(8,128)}), f32[2,16,16,1024]{3,2,1,0:T(8,128)}, u32[]{:S(2)}, u32[]{:S(2)}) async-start(f32[2,16,16,1024]{3,2,1,0:T(8,128)} %pad_maximum_fusion.1), calls=%async_computation.3 | async-start | bytes 4194304 | tf_op jit(solution)/shard_map/all_to_all | solution.py:16
  230.6 26.2 %collective-permute-start.2 = (f32[32,16,384]{2,1,0:T(8,128)}, f32[32,16,384]{2,1,0:T(8,128)}, u32[]{:S(2)}, u32[]{:S(2)}) collective-permute-start(f32[32,16,384]{2,1,0:T(8,128)} %get-tuple-element.214), channel_id=1, source_target_pairs={{0,2},{2,4},{4,6},{6,8},{8,10},{10,12},{12,14},{14,16},{16,18},{18... | collective-permute-start | bytes 2359304 | tf_op jit(solution)/shard_map/ppermute | solution.py:28
  232.8 24.0 %collective-permute-start.3 = (f32[32,16,384]{2,1,0:T(8,128)S(1)}, f32[32,16,384]{2,1,0:T(8,128)}, u32[]{:S(2)}, u32[]{:S(2)}) collective-permute-start(f32[32,16,384]{2,1,0:T(8,128)S(1)} %get-tuple-element.215), channel_id=1, source_target_pairs={{2,0},{4,2},{6,4},{8,6},{10,8},{12,10},{14,12},{16,14},{18,16},{20... | collective-permute-start | bytes 2359304 | tf_op jit(solution)/shard_map/ppermute | solution.py:29
  252.1 4.8 copy-start.26
  360.9 3.1 copy-start.2
  399.0 27.6 %all-to-all-start.5 = ((f32[2,16,16,1024]{3,2,1,0:T(8,128)}), f32[2,16,16,1024]{3,2,1,0:T(8,128)}, u32[]{:S(2)}, u32[]{:S(2)}) async-start(f32[2,16,16,1024]{3,2,1,0:T(8,128)} %pad_maximum_fusion.2), calls=%async_computation.5 | async-start | bytes 4194304 | tf_op jit(solution)/shard_map/all_to_all | solution.py:16
  406.2 25.1 %collective-permute-start.4 = (f32[32,16,384]{2,1,0:T(8,128)}, f32[32,16,384]{2,1,0:T(8,128)}, u32[]{:S(2)}, u32[]{:S(2)}) collective-permute-start(f32[32,16,384]{2,1,0:T(8,128)} %get-tuple-element.210), channel_id=1, source_target_pairs={{0,2},{2,4},{4,6},{6,8},{8,10},{10,12},{12,14},{14,16},{16,18},{18... | collective-permute-start | bytes 2359304 | tf_op jit(solution)/shard_map/ppermute | solution.py:28
  408.4 22.9 %collective-permute-start.5 = (f32[32,16,384]{2,1,0:T(8,128)S(1)}, f32[32,16,384]{2,1,0:T(8,128)}, u32[]{:S(2)}, u32[]{:S(2)}) collective-permute-start(f32[32,16,384]{2,1,0:T(8,128)S(1)} %get-tuple-element.211), channel_id=1, source_target_pairs={{2,0},{4,2},{6,4},{8,6},{10,8},{12,10},{14,12},{16,14},{18,16},{20... | collective-permute-start | bytes 2359304 | tf_op jit(solution)/shard_map/ppermute | solution.py:29
  426.5 4.8 copy-start.3
  538.6 3.0 copy-start.22
  576.7 27.5 %all-to-all-start.7 = ((f32[2,16,16,1024]{3,2,1,0:T(8,128)}), f32[2,16,16,1024]{3,2,1,0:T(8,128)}, u32[]{:S(2)}, u32[]{:S(2)}) async-start(f32[2,16,16,1024]{3,2,1,0:T(8,128)} %pad_maximum_fusion.3), calls=%async_computation.7 | async-start | bytes 4194304 | tf_op jit(solution)/shard_map/all_to_all | solution.py:16
  583.9 25.1 %collective-permute-start.6 = (f32[32,16,384]{2,1,0:T(8,128)}, f32[32,16,384]{2,1,0:T(8,128)}, u32[]{:S(2)}, u32[]{:S(2)}) collective-permute-start(f32[32,16,384]{2,1,0:T(8,128)} %get-tuple-element.206), channel_id=1, source_target_pairs={{0,2},{2,4},{4,6},{6,8},{8,10},{10,12},{12,14},{14,16},{16,18},{18... | collective-permute-start | bytes 2359304 | tf_op jit(solution)/shard_map/ppermute | solution.py:28
  586.1 22.9 %collective-permute-start.7 = (f32[32,16,384]{2,1,0:T(8,128)S(1)}, f32[32,16,384]{2,1,0:T(8,128)}, u32[]{:S(2)}, u32[]{:S(2)}) collective-permute-start(f32[32,16,384]{2,1,0:T(8,128)S(1)} %get-tuple-element.207), channel_id=1, source_target_pairs={{2,0},{4,2},{6,4},{8,6},{10,8},{12,10},{14,12},{16,14},{18,16},{20... | collective-permute-start | bytes 2359304 | tf_op jit(solution)/shard_map/ppermute | solution.py:29
  604.2 4.8 copy-start.4
  604.2 4.8 copy-start.23
  719.6 3.0 copy-start.24
  725.2 6.2 copy-start.35
  725.2 29.6 %all-to-all-start.8 = ((f32[32,16,1024]{2,1,0:T(8,128)}), f32[32,16,1024]{2,1,0:T(8,128)}, u32[]{:S(2)}, u32[]{:S(2)}) async-start(f32[32,16,1024]{2,1,0:T(8,128)} %copy.128), calls=%async_computation.8 | async-start | bytes 4194304 | tf_op jit(solution)/shard_map/all_to_all | solution.py:99
  763.0 5.0 copy-start.34
  763.0 28.2 %all-to-all-start.9 = ((f32[2,16,16,1024]{3,2,1,0:T(8,128)}), f32[2,16,16,1024]{3,2,1,0:T(8,128)}, u32[]{:S(2)}, u32[]{:S(2)}) async-start(f32[2,16,16,1024]{3,2,1,0:T(8,128)} %pad_maximum_fusion.4), calls=%async_computation.9 | async-start | bytes 4194304 | tf_op jit(solution)/shard_map/all_to_all | solution.py:16
  771.0 24.9 %collective-permute-start.8 = (f32[32,16,384]{2,1,0:T(8,128)}, f32[32,16,384]{2,1,0:T(8,128)}, u32[]{:S(2)}, u32[]{:S(2)}) collective-permute-start(f32[32,16,384]{2,1,0:T(8,128)} %get-tuple-element.202), channel_id=1, source_target_pairs={{0,2},{2,4},{4,6},{6,8},{8,10},{10,12},{12,14},{14,16},{16,18},{18... | collective-permute-start | bytes 2359304 | tf_op jit(solution)/shard_map/ppermute | solution.py:28
  773.2 22.8 %collective-permute-start.9 = (f32[32,16,384]{2,1,0:T(8,128)S(1)}, f32[32,16,384]{2,1,0:T(8,128)}, u32[]{:S(2)}, u32[]{:S(2)}) collective-permute-start(f32[32,16,384]{2,1,0:T(8,128)S(1)} %get-tuple-element.203), channel_id=1, source_target_pairs={{2,0},{4,2},{6,4},{8,6},{10,8},{12,10},{14,12},{16,14},{18,16},{20... | collective-permute-start | bytes 2359304 | tf_op jit(solution)/shard_map/ppermute | solution.py:29
  791.2 4.8 copy-start.5
  791.2 4.8 copy-start.13
  929.1 7.2 copy-start.6
  929.1 7.2 copy-start.12
  929.1 7.2 copy-start.14
  929.1 7.2 copy-start.27
  936.3 8.0 copy-start.1
  (6 other events, 12.3 us)
